TPU v7x, 32 devices: a whole 2x2x4 slice. The times are simulated.
32 devices in a mesh: ga: 2 (over y), gx: 4 (over z), gy: 2 (over x), col: 2 (over core).
Axes of the slice: x: 2, y: 2, z: 4, core: 2. Of those that a mesh axis runs over, the one named last changes fastest.
Arguments:
- pair_rep: bfloat16 [2, 160, 160, 128], P('ga', 'gx', 'gy'), parts along dimension 0, may hold values from -6 to 6
- pair_mask: int32 [2, 160, 160], P('ga', 'gx', 'gy'), parts along dimension 0, may hold values 0 or 1
- amax_history: float32 [2, 128], P(None, 'col'), may hold values from 0.3 to 3
- in_gain: float32 [128], replicated, may hold values from 0.5 to 1.5
- in_bias: float32 [128], replicated, may hold values from -3 to 3
- proj_weight: bfloat16 [128, 4, 128], P(None, None, 'col'), may hold values from -0.5 to 0.5
- gate_weight: bfloat16 [128, 128], P(None, 'col'), may hold values from -0.5 to 0.5
- out_gain: float32 [128], replicated, may hold values from 0.5 to 1.5
- out_bias: float32 [128], replicated, may hold values from -3 to 3
- out_weight: bfloat16 [128, 128], P(None, 'col'), may hold values from -0.5 to 0.5
Outputs:
- update: bfloat16 [2, 160, 160, 128], P('ga', 'gx', 'gy', 'col'), parts along dimension 0
- new_amax: float32 [4, 128], P('ga', 'col'), parts along dimension 0
There are 2 independent parts, one for each index of `ga`. A program takes and returns all parts, laid end to end along the dimension named above; an argument that names none is the same for every part. Nothing has to cross between parts.
All inputs are finite; a program needn't handle non-finite values. No bound on the sum of `pair_mask` on one device may be relied on, other than what follows from the above.
Results may differ from a plain program's by a relative error of at most 0.0065.
Values may be sent and summed in bfloat16 or wider, within the bound.
A program may use at most 128 MiB of HBM per device.

v0:
```python
import jax
import jax.numpy as jnp
from jax import lax
from jax.sharding import PartitionSpec as P

epsilon = 1e-05
format_limit = 448.0


def broadcast(block, axis, holder):
    block = jnp.where(lax.axis_index(axis) == holder, block, jnp.zeros_like(block))
    return lax.psum(block, axis)


def layer_norm(values, gain, bias):
    average = jnp.mean(values, axis=-1, keepdims=True)
    spread = jnp.mean(jnp.square(values - average), axis=-1, keepdims=True)
    return (values - average) * lax.rsqrt(spread + epsilon) * gain + bias


def crop_triangle(left_q, right_q):
    wide_rows = lax.all_gather(right_q, "gy", axis=2, tiled=True)
    row_ratio = lax.axis_size("gx") // lax.axis_size("gy")
    first_root = lax.axis_index("gy") * row_ratio
    received = [
        broadcast(wide_rows, "gx", first_root + offset_step) for offset_step in range(row_ratio)
    ]
    panel = jnp.concatenate(received, axis=1)
    return jnp.einsum(
        "cik,cjk->cij",
        lax.all_gather(left_q, "gy", axis=2, tiled=True),
        panel,
        preferred_element_type=jnp.float32,
    )


def on_device(
    pair_rep,
    pair_mask,
    amax_history,
    in_gain,
    in_bias,
    proj_weight,
    gate_weight,
    out_gain,
    out_bias,
    out_weight,
):
    normed = layer_norm(pair_rep.astype(jnp.float32), in_gain, in_bias).astype(jnp.bfloat16)
    projected = jnp.einsum(
        "bikd,dsc->scbik", normed, proj_weight, preferred_element_type=jnp.float32
    )
    masking = pair_mask.astype(jnp.float32)[None]
    left_proj = masking * jax.nn.sigmoid(projected[1]) * projected[0]
    right_proj = masking * jax.nn.sigmoid(projected[3]) * projected[2]
    local_max = jnp.stack(
        [jnp.max(jnp.abs(left_proj), axis=(1, 2, 3)), jnp.max(jnp.abs(right_proj), axis=(1, 2, 3))]
    )
    new_amax = lax.pmax(local_max, ("gx", "gy"))
    scales = amax_history / format_limit
    left_q = jnp.clip(
        left_proj / scales[0][:, None, None, None], -format_limit, format_limit
    ).astype(jnp.bfloat16)
    right_q = jnp.clip(
        right_proj / scales[1][:, None, None, None], -format_limit, format_limit
    ).astype(jnp.bfloat16)
    products = jnp.stack([crop_triangle(left_q[:, 0], right_q[:, 0])], axis=1)
    triangle = (products * (scales[0] * scales[1])[:, None, None, None]).astype(jnp.bfloat16)
    gathered = lax.all_gather(triangle, "col", axis=0, tiled=True).astype(jnp.float32)
    average = jnp.mean(gathered, axis=0, keepdims=True)
    spread = jnp.mean(jnp.square(gathered - average), axis=0, keepdims=True)
    tnorm = (
        (gathered - average) * lax.rsqrt(spread + epsilon) * out_gain[:, None, None, None]
        + out_bias[:, None, None, None]
    ).astype(jnp.bfloat16)
    mixing = jnp.einsum("cbij,cd->bijd", tnorm, out_weight, preferred_element_type=jnp.float32)
    gating = jax.nn.sigmoid(
        jnp.einsum("bijd,dc->bijc", normed, gate_weight, preferred_element_type=jnp.float32)
    )
    update = (gating * mixing).astype(jnp.bfloat16)
    return (update, new_amax)


def solution(mesh):
    placed = (
        P("ga", "gx", "gy", None),
        P("ga", "gx", "gy"),
        P(None, "col"),
        P(),
        P(),
        P(None, None, "col"),
        P(None, "col"),
        P(),
        P(),
        P(None, "col"),
    )
    return jax.shard_map(
        on_device,
        mesh=mesh,
        in_specs=placed,
        out_specs=(P("ga", "gx", "gy", "col"), P("ga", "col")),
        check_vma=False,
    )
```

profile of v0, /device:TPU:0, one launch (start us, length us, event | category | flops | bytes accessed | tf_op | source)
XLA Modules:
  0.0 166.5 jit_solution(14759591514947378513)
XLA Ops:
  7.3 0.8 broadcast_multiply_fusion.2
  8.0 0.7 convert_bitcast_fusion.1
  8.8 1.6 convert_reduce_fusion.1
  10.4 1.2 fusion.13
  11.6 2.1 %convolution_bitcast_fusion = f32[4,64,40,80]{3,1,0,2:T(8,128)S(1)} fusion(bf16[1,40,80,128]{3,2,1,0:T(8,128)(2,1)S(1)} %copy-done.2, f32[128]{0:T(128)S(1)} %copy-done.6, f32[128]{0:T(128)S(1)} %copy-done.7, f32[40,80]{1,0:T(8,128)S(1)} %add_rsqrt_fusion.1, f32[40,80]{1,0:T(8,128)S(1)} %broadcast_multiply_fusion.1, bf16[128,4,64]{0,2,1:T(8,128)(2,1)S(1)} %copy-done), kind=kOutput, calls=%fused_computation.13 | convolution fusion | flops 212172800 | bytes 4188160 | tf_op jit(solution)/shard_map/bikd,dsc->scbik/dot_general | solution.py:50
  13.7 2.3 %fusion.45 = (bf16[64,40,80]{2,0,1:T(8,128)(2,1)S(1)}, bf16[64,40,80]{2,0,1:T(8,128)(2,1)}) fusion(f32[4,64,40,80]{3,1,0,2:T(8,128)S(1)} %convolution_bitcast_fusion, f32[64]{0:T(128)S(1)} %get-tuple-element.10, f32[40,80]{1,0:T(8,128)S(1)} %convert_bitcast_fusion.1, f32[64]{0:T(128)S(1)} %get-tuple-element.11), kind=kLoop, calls=%fused_computation.56 | loop fusion | flops 3276800 | bytes 4109312 | tf_op jit(solution)/shard_map/convert_element_type | solution.py:66
  16.3 0.5 copy.22
  16.7 21.9 %all_gather.10 = bf16[64,40,160]{0,1,2:T(8,128)(2,1)S(1)} all-gather(bf16[64,40,80]{0,1,2:T(8,128)(2,1)S(1)} %copy.22), channel_id=1, replica_groups=mesh['ga'=2,'gx'=4,'gy'=2,'col'=2] {'gy'}, dimensions={2}, use_global_device_ids=true | all-gather | bytes 1228800 | tf_op jit(solution)/shard_map/all_gather | solution.py:22
  38.6 4.0 %copy.23 = bf16[64,40,160]{2,1,0:T(8,128)(2,1)} copy(bf16[64,40,160]{0,1,2:T(8,128)(2,1)S(1)} %all_gather.10) | data formatting | bytes 1638400 | tf_op jit(solution)/shard_map/all_gather | solution.py:22
  42.6 3.0 %broadcast_select_fusion.1 = (bf16[64,40,160]{2,1,0:T(8,128)(2,1)}, bf16[64,40,160]{2,1,0:T(8,128)(2,1)}) fusion(bf16[64,40,160]{2,1,0:T(8,128)(2,1)} %copy.23, pred[]{:T(512)S(6)} %eq.6, pred[]{:T(512)S(6)} %eq.7), kind=kLoop, calls=%fused_computation.61 | loop fusion | flops 819200 | bytes 2457602 | tf_op jit(solution)/shard_map/jit(_where)/select_n | solution.py:11
  45.7 1.1 copy-done.3
  46.8 0.5 copy.20
  47.2 20.1 %all_gather.9 = bf16[64,40,160]{0,1,2:T(8,128)(2,1)S(1)} all-gather(bf16[64,40,80]{0,1,2:T(8,128)(2,1)S(1)} %copy.20), channel_id=1, replica_groups=mesh['ga'=2,'gx'=4,'gy'=2,'col'=2] {'gy'}, dimensions={2}, use_global_device_ids=true | all-gather | bytes 1228800 | tf_op jit(solution)/shard_map/all_gather | solution.py:31
  67.3 4.0 %copy.25 = bf16[64,40,160]{2,1,0:T(8,128)(2,1)} copy(bf16[64,40,160]{0,1,2:T(8,128)(2,1)S(1)} %all_gather.9) | data formatting | bytes 1638400 | tf_op jit(solution)/shard_map/all_gather | solution.py:31
  71.4 3.5 %fusion.37 = (f32[64]{0:T(128)S(1)}, f32[64]{0:T(128)S(1)}) fusion(f32[4,64,40,80]{3,1,0,2:T(8,128)} %copy-done.1, f32[40,80]{1,0:T(8,128)S(1)} %convert_bitcast_fusion.1), kind=kLoop, calls=%fused_computation.43 | loop fusion | flops 2867072 | bytes 3290112 | tf_op jit(solution)/shard_map/reduce_max | solution.py:57
  74.9 23.4 %pmax.7 = f32[2,64]{1,0:T(2,128)} all-reduce(f32[2,64]{1,0:T(2,128)S(1)} %pad_maximum_fusion), channel_id=1, replica_groups=mesh['ga'=2,'gx'=4,'gy'=2,'col'=2] {'gx','gy'}, use_global_device_ids=true, to_apply=%region_8.9 | all-reduce | flops 128 | bytes 1024 | tf_op jit(solution)/shard_map/pmax | solution.py:59
  98.2 0.5 fusion.58
  98.7 2.0 %fusion.22 = f32[40,80,64]{1,2,0:T(8,128)S(1)} fusion(bf16[1,40,80,128]{3,2,1,0:T(8,128)(2,1)S(1)} %copy-done.2, f32[128]{0:T(128)S(1)} %copy-done.6, f32[128]{0:T(128)S(1)} %copy-done.7, f32[40,80]{1,0:T(8,128)S(1)} %add_rsqrt_fusion.1, f32[40,80]{1,0:T(8,128)S(1)} %broadcast_multiply_fusion.1, bf16[128,64]{0,1:T(8,128)(2,1)} %param.16), kind=kOutput, calls=%fused_computation.27 | convolution fusion | flops 55500800 | bytes 1681408 | tf_op jit(solution)/shard_map/bijd,dc->bijc/dot_general | solution.py:78
  100.7 51.0 %all-reduce.3.cloned.1.call-done = (bf16[64,40,160]{2,1,0:T(8,128)(2,1)}, bf16[64,40,160]{2,1,0:T(8,128)(2,1)}) async-done(((bf16[64,40,160]{2,1,0:T(8,128)(2,1)}, bf16[64,40,160]{2,1,0:T(8,128)(2,1)}), (bf16[64,40,160]{2,1,0:T(8,128)(2,1)}, bf16[64,40,160]{2,1,0:T(8,128)(2,1)})) %all-reduce.3.cloned.1.call-update) | async-done | bytes 1638416 | tf_op jit(solution)/shard_map/psum | solution.py:12
  151.7 2.5 %fusion.24 = bf16[64,40,80]{2,1,0:T(8,128)(2,1)S(1)} fusion(bf16[64,40,160]{2,1,0:T(8,128)(2,1)S(1)} %copy-done.4, bf16[64,40,160]{2,1,0:T(8,128)(2,1)} %get-tuple-element.4, bf16[64,40,160]{2,1,0:T(8,128)(2,1)} %get-tuple-element.5, f32[64]{0:T(128)} %fusion.58), kind=kOutput, calls=%fused_computation.29 | convolution fusion | flops 69222400 | bytes 2867456 | tf_op jit(solution)/shard_map/cik,cjk->cij/dot_general | solution.py:29
  154.2 2.7 %all-gather = bf16[128,40,80]{2,1,0:T(8,128)(2,1)S(1)} all-gather(bf16[64,40,80]{2,1,0:T(8,128)(2,1)S(1)} %fusion.24), channel_id=2, replica_groups=mesh['ga'=2,'gx'=4,'gy'=2,'col'=2] {'col'}, dimensions={0}, use_global_device_ids=true | all-gather | bytes 1228800 | tf_op jit(solution)/shard_map/all_gather | solution.py:69
  157.3 0.5 fusion.3
  157.8 0.5 fusion.27
  158.5 1.2 fusion.47
  (28 shorter events, 0.8 us)
Async XLA Ops:
  7.2 4.4 %copy-start = (bf16[128,4,64]{0,2,1:T(8,128)(2,1)S(1)}, bf16[128,4,64]{0,2,1:T(8,128)(2,1)}, u32[]{:S(2)}) copy-start(bf16[128,4,64]{0,2,1:T(8,128)(2,1)} %param.15) | copy-start | bytes 196612
  7.2 3.2 %copy-start.2 = (bf16[1,40,80,128]{3,2,1,0:T(8,128)(2,1)S(1)}, bf16[1,40,80,128]{3,2,1,0:T(8,128)(2,1)}, u32[]{:S(2)}) copy-start(bf16[1,40,80,128]{3,2,1,0:T(8,128)(2,1)} %param.10) | copy-start | bytes 2457604
  7.2 4.4 %copy-start.6 = (f32[128]{0:T(128)S(1)}, f32[128]{0:T(128)}, u32[]{:S(2)}) copy-start(f32[128]{0:T(128)} %param.14) | copy-start | bytes 1540
  7.2 4.4 %copy-start.7 = (f32[128]{0:T(128)S(1)}, f32[128]{0:T(128)}, u32[]{:S(2)}) copy-start(f32[128]{0:T(128)} %param.13) | copy-start | bytes 1540
  7.2 144.5 %all-reduce.3.cloned.1.call-start = ((), (), s32[]{:S(2)}) async-start(), calls=%async_computation | async-start | bytes 5242880 | tf_op jit(solution)/shard_map/psum | solution.py:12
  13.7 2.5 %copy-start.1 = (f32[4,64,40,80]{3,1,0,2:T(8,128)}, f32[4,64,40,80]{3,1,0,2:T(8,128)S(1)}, u32[]{:S(2)}) copy-start(f32[4,64,40,80]{3,1,0,2:T(8,128)S(1)} %convolution_bitcast_fusion) | copy-start | bytes 9830404
  45.7 1.1 copy-start.3
  98.7 53.0 %copy-start.4 = (bf16[64,40,160]{2,1,0:T(8,128)(2,1)S(1)}, bf16[64,40,160]{2,1,0:T(8,128)(2,1)}, u32[]{:S(2)}) copy-start(bf16[64,40,160]{2,1,0:T(8,128)(2,1)} %copy.25) | copy-start | bytes 2457604
  157.0 0.8 copy-start.8
  157.0 0.8 copy-start.9
  157.8 0.7 copy-start.5
Sparse Core Ops, SparseCore 0:
  45.8 105.8 all-reduce.2
where the time goes:
time: 167 us
  blocking collectives  68.1 us (41%)
  waiting for transfers between devices  51 us (31%)
  other arithmetic  14.9 us (9%)
  between operations  14.2 us (9%)
  local copies, waits for them, and re-layouts  10.5 us (6%)
  matrix products  7.79 us (5%)
    psum x1, waiting for transfers between devices, broadcast(): return lax.psum(block, axis)  51 us
    pmax x1, blocking collectives, on_device(): new_amax = lax.pmax(local_max, ('gx', 'gy'))  23.4 us
    all_gather x1, blocking collectives, crop_triangle(): wide_rows = lax.all_gather(right_q, 'gy', axis=2, tiled=True)  21.9 us
    all_gather x1, blocking collectives, crop_triangle(): lax.all_gather(left_q, 'gy', axis=2, tiled=True)  20.1 us
    all_gather x1, local copies, waits for them, and re-layouts, crop_triangle(): lax.all_gather(left_q, 'gy', axis=2, tiled=True)  4.05 us
    all_gather x1, local copies, waits for them, and re-layouts, crop_triangle(): wide_rows = lax.all_gather(right_q, 'gy', axis=2, tiled=True)  4.02 us
    reduce_max x1, other arithmetic, on_device(): jnp.max(jnp.abs(left_proj), axis=(1, 2, 3))  3.47 us
  transfers between devices with their start and end apart: 1, of which 1 were waited for; matrix products, arithmetic and copies ran while one was open for 6% of the time, Pallas kernels for 0%

commit v1 on v0

--- a/solution.py
+++ b/solution.py
@@ -9,7 +9,7 @@
 
 def broadcast(block, axis, holder):
     block = jnp.where(lax.axis_index(axis) == holder, block, jnp.zeros_like(block))
-    return lax.psum(block, axis)
+    return jnp.sum(lax.all_gather(block, axis), axis=0)
 
 
 def layer_norm(values, gain, bias):

time: 167 us -> 264 us (1.58)
  waiting for transfers between devices: 51 us -> 134 us
  other arithmetic: 14.9 us -> 22.7 us
  local copies, waits for them, and re-layouts: 10.5 us -> 15.7 us
    all_gather x0 -> x2, waiting for transfers between devices: none -> 134 us  [broadcast(): return jnp.sum(lax.all_gather(block, axis), axis=0)]
    psum x1 -> x0, waiting for transfers between devices: 51 us -> none  [broadcast(): return lax.psum(block, axis)]
    reduce_sum x0 -> x2, other arithmetic: none -> 9.83 us  [broadcast(): return jnp.sum(lax.all_gather(block, axis), axis=0)]
    select_n x0 -> x2, local copies, waits for them, and re-layouts: none -> 9.29 us  [broadcast(): jnp.where(lax.axis_index(axis) == holder, block, jnp.zeros_like(block))]
    all_gather x1 -> x0, local copies, waits for them, and re-layouts: 4.02 us -> none  [crop_triangle(): wide_rows = lax.all_gather(right_q, 'gy', axis=2, tiled=True)]
  transfers between devices with their start and end apart: 1 -> 2, of which waited for: 1 -> 2; matrix products, arithmetic and copies ran while one was open for 6% -> 7% of each run, Pallas kernels for 0% -> 0%
where the time goes in v1:
time: 264 us; the launch traced here: 263 us
  waiting for transfers between devices  134 us (51%)
  blocking collectives  68.1 us (26%)
  other arithmetic  22.7 us (9%)
  local copies, waits for them, and re-layouts  15.7 us (6%)
  between operations  14.2 us (5%)
  matrix products  7.67 us (3%)
    all_gather x2, waiting for transfers between devices, broadcast(): return jnp.sum(lax.all_gather(block, axis), axis=0)  134 us
    pmax x1, blocking collectives, on_device(): new_amax = lax.pmax(local_max, ('gx', 'gy'))  23.4 us
    all_gather x1, blocking collectives, crop_triangle(): wide_rows = lax.all_gather(right_q, 'gy', axis=2, tiled=True)  21.9 us
    all_gather x1, blocking collectives, crop_triangle(): lax.all_gather(left_q, 'gy', axis=2, tiled=True)  20.1 us
    reduce_sum x2, other arithmetic, broadcast(): return jnp.sum(lax.all_gather(block, axis), axis=0)  9.83 us
    select_n x2, local copies, waits for them, and re-layouts, broadcast(): jnp.where(lax.axis_index(axis) == holder, block, jnp.zeros_like(block))  9.29 us
  transfers between devices with their start and end apart: 2, of which 2 were waited for; matrix products, arithmetic and copies ran while one was open for 7% of the time, Pallas kernels for 0%

profile of v1, /device:TPU:0, one launch (start us, length us, event | category | flops | bytes accessed | tf_op | source)
XLA Modules:
  0.0 263.0 jit_solution(6233949567339225766)
XLA Ops:
  7.3 0.8 broadcast_multiply_fusion.2
  8.0 0.7 convert_bitcast_fusion.1
  8.8 1.6 convert_reduce_fusion.1
  10.4 1.2 fusion.13
  11.6 2.1 convolution_bitcast_fusion
  13.7 2.4 fusion.45
  16.8 21.9 %all_gather.22 = bf16[64,40,160]{0,1,2:T(8,128)(2,1)S(1)} all-gather(bf16[64,40,80]{0,1,2:T(8,128)(2,1)S(1)} %copy.45), channel_id=1, replica_groups=mesh['ga'=2,'gx'=4,'gy'=2,'col'=2] {'gy'}, dimensions={2}, use_global_device_ids=true | all-gather | bytes 1228800 | tf_op jit(solution)/shard_map/all_gather | solution.py:22
  38.7 1.4 broadcast_select_fusion.1
  40.1 5.2 %copy.46 = bf16[64,40,160]{2,1,0:T(8,128)(2,1)} copy(bf16[64,40,160]{0,1,2:T(8,128)(2,1)} %get-tuple-element.6) | data formatting | bytes 1638400 | tf_op jit(solution)/shard_map/jit(_where)/select_n | solution.py:11
  45.4 4.1 %copy.48 = bf16[64,40,160]{2,1,0:T(8,128)(2,1)} copy(bf16[64,40,160]{0,1,2:T(8,128)(2,1)S(1)} %get-tuple-element.7) | data formatting | bytes 1638400 | tf_op jit(solution)/shard_map/jit(_where)/select_n | solution.py:11
  49.5 1.1 copy-done.3
  51.0 20.1 %all_gather.21 = bf16[64,40,160]{0,1,2:T(8,128)(2,1)S(1)} all-gather(bf16[64,40,80]{0,1,2:T(8,128)(2,1)S(1)} %copy.43), channel_id=1, replica_groups=mesh['ga'=2,'gx'=4,'gy'=2,'col'=2] {'gy'}, dimensions={2}, use_global_device_ids=true | all-gather | bytes 1228800 | tf_op jit(solution)/shard_map/all_gather | solution.py:31
  71.1 4.0 %copy.52 = bf16[64,40,160]{2,1,0:T(8,128)(2,1)} copy(bf16[64,40,160]{0,1,2:T(8,128)(2,1)S(1)} %all_gather.21) | data formatting | bytes 1638400 | tf_op jit(solution)/shard_map/all_gather | solution.py:31
  75.1 3.5 %fusion.37 = (f32[64]{0:T(128)S(1)}, f32[64]{0:T(128)S(1)}) fusion(f32[4,64,40,80]{3,1,0,2:T(8,128)} %copy-done.1, f32[40,80]{1,0:T(8,128)S(1)} %convert_bitcast_fusion.1), kind=kLoop, calls=%fused_computation.45 | loop fusion | flops 2867072 | bytes 3290112 | tf_op jit(solution)/shard_map/reduce_max | solution.py:57
  78.6 23.4 %pmax.7 = f32[2,64]{1,0:T(2,128)} all-reduce(f32[2,64]{1,0:T(2,128)S(1)} %pad_maximum_fusion), channel_id=1, replica_groups=mesh['ga'=2,'gx'=4,'gy'=2,'col'=2] {'gx','gy'}, use_global_device_ids=true, to_apply=%region_8.9 | all-reduce | flops 128 | bytes 1024 | tf_op jit(solution)/shard_map/pmax | solution.py:59
  102.0 1.9 fusion.22
  103.9 41.3 %all-gather.6.cloned.1.call-done = bf16[256,40,160]{2,1,0:T(8,128)(2,1)} async-done(((bf16[64,40,160]{2,1,0:T(8,128)(2,1)}), bf16[256,40,160]{2,1,0:T(8,128)(2,1)}) %all-gather.6.cloned.1.call-update) | async-done | bytes 3276816 | tf_op jit(solution)/shard_map/all_gather | solution.py:12
  145.1 4.9 %reduce_sum.62 = bf16[64,40,160]{2,1,0:T(8,128)(2,1)} reduce(bf16[4,64,40,160]{3,2,1,0:T(8,128)(2,1)} %bitcast.131, bf16[]{:T(256)} %constant.38.clone.1), dimensions={0}, to_apply=%region_2.0 | reduce | flops 1228800 | bytes 4096002 | tf_op jit(solution)/shard_map/reduce_sum | solution.py:12
  150.0 93.2 %all-gather.8.cloned.1.call-done = bf16[256,40,160]{2,1,0:T(8,128)(2,1)} async-done(((bf16[64,40,160]{2,1,0:T(8,128)(2,1)}), bf16[256,40,160]{2,1,0:T(8,128)(2,1)}) %all-gather.8.cloned.1.call-update) | async-done | bytes 3276816 | tf_op jit(solution)/shard_map/all_gather | solution.py:12
  243.2 4.9 %reduce_sum.63 = bf16[64,40,160]{2,1,0:T(8,128)(2,1)} reduce(bf16[4,64,40,160]{3,2,1,0:T(8,128)(2,1)} %bitcast.132, bf16[]{:T(256)} %constant.38.clone.1), dimensions={0}, to_apply=%region_3.0 | reduce | flops 1228800 | bytes 4096002 | tf_op jit(solution)/shard_map/reduce_sum | solution.py:12
  248.2 2.5 fusion.24
  250.7 2.7 %all-gather.2 = bf16[128,40,80]{2,1,0:T(8,128)(2,1)S(1)} all-gather(bf16[64,40,80]{2,1,0:T(8,128)(2,1)S(1)} %fusion.24), channel_id=4, replica_groups=mesh['ga'=2,'gx'=4,'gy'=2,'col'=2] {'col'}, dimensions={0}, use_global_device_ids=true | all-gather | bytes 1228800 | tf_op jit(solution)/shard_map/all_gather | solution.py:69
  254.3 0.5 fusion.27
  255.0 1.2 fusion.47
  (36 shorter events, 2.3 us)
Async XLA Ops:
  7.2 4.4 %copy-start = (bf16[128,4,64]{0,2,1:T(8,128)(2,1)S(1)}, bf16[128,4,64]{0,2,1:T(8,128)(2,1)}, u32[]{:S(2)}) copy-start(bf16[128,4,64]{0,2,1:T(8,128)(2,1)} %param.15) | copy-start | bytes 196612
  7.2 3.2 %copy-start.2 = (bf16[1,40,80,128]{3,2,1,0:T(8,128)(2,1)S(1)}, bf16[1,40,80,128]{3,2,1,0:T(8,128)(2,1)}, u32[]{:S(2)}) copy-start(bf16[1,40,80,128]{3,2,1,0:T(8,128)(2,1)} %param.10) | copy-start | bytes 2457604
  7.2 4.4 %copy-start.6 = (f32[128]{0:T(128)S(1)}, f32[128]{0:T(128)}, u32[]{:S(2)}) copy-start(f32[128]{0:T(128)} %param.14) | copy-start | bytes 1540
  7.2 4.4 %copy-start.7 = (f32[128]{0:T(128)S(1)}, f32[128]{0:T(128)}, u32[]{:S(2)}) copy-start(f32[128]{0:T(128)} %param.13) | copy-start | bytes 1540
  7.2 137.9 %all-gather.6.cloned.1.call-start = ((), (), s32[]{:S(2)}) async-start(), calls=%async_computation | async-start | bytes 6553600 | tf_op jit(solution)/shard_map/all_gather | solution.py:12
  13.7 2.6 copy-start.1
  45.3 197.9 %all-gather.8.cloned.1.call-start = ((), (), s32[]{:S(2)}) async-start(), calls=%async_computation.1 | async-start | bytes 6553600 | tf_op jit(solution)/shard_map/all_gather | solution.py:12
  49.4 1.1 copy-start.3
  75.1 26.9 %copy-start.10 = (bf16[128,64]{0,1:T(8,128)(2,1)S(1)}, bf16[128,64]{0,1:T(8,128)(2,1)}, u32[]{:S(2)}) copy-start(bf16[128,64]{0,1:T(8,128)(2,1)} %param.16) | copy-start | bytes 49156
  243.2 4.9 %copy-start.4 = (bf16[64,40,160]{2,1,0:T(8,128)(2,1)S(1)}, bf16[64,40,160]{2,1,0:T(8,128)(2,1)}, u32[]{:S(2)}) copy-start(bf16[64,40,160]{2,1,0:T(8,128)(2,1)} %copy.52) | copy-start | bytes 2457604
  253.5 0.8 copy-start.8
  253.5 0.8 copy-start.9
  254.3 0.7 copy-start.5
Sparse Core Ops, SparseCore 0:
  45.4 99.6 all-gather.5
  146.7 96.4 all-gather.7
